TPU v7x, 32 devices: a whole 2x2x4 slice. The times are simulated.
32 devices in a mesh: fsdp: 4 (over y, x), ep: 8 (over z, core).
Axes of the slice: x: 2, y: 2, z: 4, core: 2. Of those that a mesh axis runs over, the one named last changes fastest.
Arguments:
- hidden_in: bfloat16 [8192, 2048], P(('fsdp', 'ep')), may hold values from -6 to 6
- norm_gain: float32 [2048], replicated, may hold values from 0.25 to 1.75
- expert_ids: int32 [8192, 8], P(('fsdp', 'ep')), may hold values from 0 to 15, all different within a row; in each aligned block of 256 rows (0 to 255, 256 to 511, ...) at most 160 rows name the same one
- expert_probs: float32 [8192, 8], P(('fsdp', 'ep')), may hold values from 0.05 to 0.25
- gate_proj: bfloat16 [16, 2048, 768], P('ep', 'fsdp'), may hold values from -0.125 to 0.125
- up_proj: bfloat16 [16, 2048, 768], P('ep', 'fsdp'), may hold values from -0.125 to 0.125
- down_proj: bfloat16 [16, 768, 2048], P('ep', None, 'fsdp'), may hold values from -0.21875 to 0.21875
Outputs:
- moe_out: bfloat16 [8192, 2048], P(('fsdp', 'ep'))
Inputs may be any that keep to these rules, and one draw needn't show every extreme that they name: `expert_ids`: within the rows of one device (aligned blocks of 256 rows) each expert id is named by at most 160 rows, and in some blocks one expert by exactly 160; the 8 ids of a row are distinct.
All inputs are finite; a program needn't handle non-finite values.
Results may differ from a plain program's by a relative error of at most 0.0025.
Values may be sent and summed in bfloat16 or wider, within the bound.
A program may use at most 128 MiB of HBM per device.

v0:
```python
import jax
import jax.numpy as jnp
from jax import lax
from jax.sharding import PartitionSpec as P


def rms_norm(hidden_in, norm_gain):
    values = hidden_in.astype(jnp.float32)
    spread = jnp.mean(values * values, axis=-1, keepdims=True)
    return (values * lax.rsqrt(spread + 1e-06) * norm_gain).astype(jnp.bfloat16)


def per_device(hidden_in, norm_gain, expert_ids, expert_probs, gate_proj, up_proj, down_proj):
    local_experts = gate_proj.shape[0]
    normed = rms_norm(hidden_in, norm_gain)
    all_experts = local_experts * lax.axis_size("ep")
    hot = expert_ids[:, :, None] == jnp.arange(all_experts, dtype=jnp.int32)
    weights = jnp.sum(jnp.where(hot, expert_probs[:, :, None], 0.0), axis=1)
    tokens = lax.all_gather(normed, "ep", axis=0, tiled=True)
    routed = lax.all_to_all(
        weights.reshape(weights.shape[0], lax.axis_size("ep"), local_experts),
        "ep",
        split_axis=1,
        concat_axis=0,
        tiled=True,
    ).reshape(tokens.shape[0], local_experts)
    total = 0.0
    gate_all = lax.all_gather(gate_proj, "fsdp", axis=1, tiled=True)
    up_all = lax.all_gather(up_proj, "fsdp", axis=1, tiled=True)
    down_all = lax.all_gather(down_proj, "fsdp", axis=2, tiled=True)
    for e in range(local_experts):
        gate = jnp.dot(tokens, gate_all[e], preferred_element_type=jnp.float32)
        up = jnp.dot(tokens, up_all[e], preferred_element_type=jnp.float32)
        act = (jax.nn.silu(gate) * up).astype(jnp.bfloat16)
        out = jnp.dot(act, down_all[e], preferred_element_type=jnp.float32).astype(jnp.bfloat16)
        total = total + out.astype(jnp.float32) * routed[:, e, None]
    combined = lax.psum_scatter(total, "ep", scatter_dimension=0, tiled=True)
    return combined.astype(jnp.bfloat16)


def solution(mesh):
    return jax.shard_map(
        per_device,
        mesh=mesh,
        in_specs=(
            P(("fsdp", "ep"), None),
            P(),
            P(("fsdp", "ep"), None),
            P(("fsdp", "ep"), None),
            P("ep", "fsdp", None),
            P("ep", "fsdp", None),
            P("ep", None, "fsdp"),
        ),
        out_specs=P(("fsdp", "ep"), None),
        check_vma=False,
    )
```

profile of v0, /device:TPU:0, one launch (start us, length us, event | category | flops | bytes accessed | tf_op | source)
XLA Modules:
  0.0 533.1 jit_solution(4729882364466384271)
XLA Ops:
  6.5 0.0 copy-start
  6.5 0.0 copy-start.1
  6.5 0.0 all-gather.7.cloned.1.call-start
  6.5 0.7 all-gather.7.cloned.1.call-update
  7.3 0.0 all-gather.5.cloned.1.call-start
  7.3 1.5 fusion.5
  8.8 2.5 fusion.7
  11.3 0.0 all-gather.5.cloned.1.call-update
  11.4 0.0 all-gather.9.cloned.1.call-start
  11.4 0.7 all-gather.9.cloned.1.call-update
  12.1 0.0 all-gather.11.cloned.1.call-start
  12.1 0.5 all-gather.11.cloned.1.call-update
  12.7 0.0 reduce-scatter.2.cloned.1.call-start
  12.7 0.0 copy-done
  12.7 0.0 copy-done.1
  12.8 11.8 %all_to_all.15 = f32[256,8,2]{0,2,1:T(2,128)S(1)} all-to-all(f32[256,8,2]{0,2,1:T(2,128)S(1)} %reshape.18), channel_id=1, replica_groups=mesh['fsdp'=4,'ep'=8] {'ep'}, dimensions={1} | all-to-all | bytes 32768 | tf_op jit(solution)/shard_map/all_to_all | solution.py:20
  24.6 57.4 %all-gather.7.cloned.1.call-done = bf16[2,2048,768]{2,1,0:T(8,128)(2,1)} async-done(((bf16[2,512,768]{2,1,0:T(8,128)(2,1)}), bf16[2,2048,768]{2,1,0:T(8,128)(2,1)}) %all-gather.7.cloned.1.call-update) | async-done | bytes 6291472 | tf_op jit(solution)/shard_map/all_gather | solution.py:28
  82.0 83.7 %all-gather.5.cloned.1.call-done = bf16[2048,2048]{1,0:T(8,128)(2,1)} async-done(((bf16[256,2048]{1,0:T(8,128)(2,1)}), bf16[2048,2048]{1,0:T(8,128)(2,1)}) %all-gather.5.cloned.1.call-update) | async-done | bytes 8388624 | tf_op jit(solution)/shard_map/all_gather | solution.py:19
  165.6 0.0 copy-start.2
  165.6 0.0 copy-start.3
  165.6 11.8 %fusion.1 = f32[2048,768]{1,0:T(8,128)} fusion(bf16[2048,2048]{1,0:T(8,128)(2,1)} %all-gather.5.cloned.1.call-done, bf16[2,2048,768]{2,1,0:T(8,128)(2,1)} %all-gather.7.cloned.1.call-done), kind=kOutput, calls=%fused_computation.7 | convolution fusion | flops 6442450944 | bytes 17825792 | tf_op jit(solution)/shard_map/dot_general | solution.py:32
  177.4 0.0 copy-done.2
  177.4 0.0 copy-done.3
  177.4 8.5 %fusion.2 = f32[2048,768]{1,0:T(8,128)} fusion(bf16[2048,2048]{1,0:T(8,128)(2,1)S(1)} %copy-done.2, bf16[2,2048,768]{2,1,0:T(8,128)(2,1)S(1)} %copy-done.3), kind=kOutput, calls=%fused_computation.11 | convolution fusion | flops 6442450944 | bytes 17825792 | tf_op jit(solution)/shard_map/dot_general | solution.py:32
  185.9 50.1 %all-gather.9.cloned.1.call-done = bf16[2,2048,768]{2,1,0:T(8,128)(2,1)} async-done(((bf16[2,512,768]{2,1,0:T(8,128)(2,1)}), bf16[2,2048,768]{2,1,0:T(8,128)(2,1)}) %all-gather.9.cloned.1.call-update) | async-done | bytes 6291472 | tf_op jit(solution)/shard_map/all_gather | solution.py:29
  236.0 71.6 %all-gather.11.cloned.1.call-done = bf16[2,768,2048]{2,1,0:T(8,128)(2,1)} async-done(((bf16[2,768,512]{2,1,0:T(8,128)(2,1)}), bf16[2,768,2048]{2,1,0:T(8,128)(2,1)}) %all-gather.11.cloned.1.call-update) | async-done | bytes 6291472 | tf_op jit(solution)/shard_map/all_gather | solution.py:30
  307.6 22.1 %fusion = bf16[2048,2048]{1,0:T(8,128)(2,1)} fusion(f32[2048,768]{1,0:T(8,128)} %fusion.2, bf16[2048,2048]{1,0:T(8,128)(2,1)} %all-gather.5.cloned.1.call-done, bf16[2,768,2048]{2,1,0:T(8,128)(2,1)} %all-gather.11.cloned.1.call-done, bf16[2,2048,768]{2,1,0:T(8,128)(2,1)} %all-gather.9.cloned.1.call-done), kind=kOutput, calls=%fused_computation.3 | convolution fusion | flops 12894339072 | bytes 29360128 | tf_op jit(solution)/shard_map/dot_general | solution.py:35
  329.7 25.8 %multiply_add_fusion = f32[2048,2048]{1,0:T(8,128)} fusion(f32[2048]{0:T(1024)S(1)} %bitcast.35, f32[2048]{0:T(1024)S(1)} %bitcast.34, bf16[2048,2048]{1,0:T(8,128)(2,1)} %fusion, f32[2048,768]{1,0:T(8,128)} %fusion.1, bf16[2048,2048]{1,0:T(8,128)(2,1)} %all-gather.5.cloned.1.call-done, bf16[2,768,2048]{2,1,0:T(8,128)(2,1)} %all-gather.11.cloned.1.call-done, ...), kind=kOutput, calls=%fused_computation | convolution fusion | flops 12919504896 | bytes 46153728 | tf_op jit(solution)/shard_map/dot_general | solution.py:35
  355.5 0.0 reduce-scatter.2.cloned.1.call-update
  355.5 168.3 %reduce-scatter.2.cloned.1.call-done = f32[256,2048]{1,0:T(8,128)} async-done(((f32[2048,2048]{1,0:T(8,128)}), f32[256,2048]{1,0:T(8,128)}) %reduce-scatter.2.cloned.1.call-update) | async-done | bytes 2097168 | tf_op jit(solution)/shard_map/reduce_scatter | solution.py:37
  523.8 2.7 convert_element_type.35
  (4 shorter events, 0.1 us)
Async XLA Ops:
  6.5 6.2 %copy-start = (f32[256,8]{0,1:T(8,128)S(1)}, f32[256,8]{0,1:T(8,128)}, u32[]{:S(2)}) copy-start(f32[256,8]{0,1:T(8,128)} %param.10) | copy-start | bytes 24580
  6.5 6.2 %copy-start.1 = (s32[256,8]{0,1:T(8,128)S(1)}, s32[256,8]{0,1:T(8,128)}, u32[]{:S(2)}) copy-start(s32[256,8]{0,1:T(8,128)} %param.9) | copy-start | bytes 24580
  6.5 75.4 %all-gather.7.cloned.1.call-start = ((), (), s32[]{:S(2)}) async-start(), calls=%async_computation.3 | async-start | bytes 7864320 | tf_op jit(solution)/shard_map/all_gather | solution.py:28
  7.3 158.4 %all-gather.5.cloned.1.call-start = ((), (), s32[]{:S(2)}) async-start(), calls=%async_computation.2 | async-start | bytes 9437184 | tf_op jit(solution)/shard_map/all_gather | solution.py:19
  11.4 224.7 %all-gather.9.cloned.1.call-start = ((), (), s32[]{:S(2)}) async-start(), calls=%async_computation.4 | async-start | bytes 7864320 | tf_op jit(solution)/shard_map/all_gather | solution.py:29
  12.1 295.5 %all-gather.11.cloned.1.call-start = ((), (), s32[]{:S(2)}) async-start(), calls=%async_computation.5 | async-start | bytes 7864320 | tf_op jit(solution)/shard_map/all_gather | solution.py:30
  12.7 511.2 %reduce-scatter.2.cloned.1.call-start = ((), (), s32[]{:S(2)}) async-start(), calls=%async_computation.6 | async-start | bytes 18874368 | tf_op jit(solution)/shard_map/reduce_scatter | solution.py:37
  165.6 11.8 %copy-start.2 = (bf16[2048,2048]{1,0:T(8,128)(2,1)S(1)}, bf16[2048,2048]{1,0:T(8,128)(2,1)}, u32[]{:S(2)}) copy-start(bf16[2048,2048]{1,0:T(8,128)(2,1)} %all-gather.5.cloned.1.call-done) | copy-start | bytes 25165828
  165.6 11.8 %copy-start.3 = (bf16[2,2048,768]{2,1,0:T(8,128)(2,1)S(1)}, bf16[2,2048,768]{2,1,0:T(8,128)(2,1)}, u32[]{:S(2)}) copy-start(bf16[2,2048,768]{2,1,0:T(8,128)(2,1)} %all-gather.7.cloned.1.call-done) | copy-start | bytes 18874372
Sparse Core Ops, SparseCore 0:
  9.2 72.7 all-gather.6
  83.6 82.0 all-gather.4
  167.5 68.5 all-gather.8
  237.7 69.8 all-gather.10
  355.6 168.1 reduce-scatter.1
where the time goes:
time: 533 us
  waiting for transfers between devices  433 us (81%)
  matrix products  68.2 us (13%)
  between operations  13.2 us (2%)
  blocking collectives  11.8 us (2%)
  other arithmetic  6.76 us (1%)
    reduce_scatter x1, waiting for transfers between devices, per_device(): combined = lax.psum_scatter(total, 'ep', scatter_dimension=0, tiled=True)  168 us
    all_gather x1, waiting for transfers between devices, per_device(): tokens = lax.all_gather(normed, 'ep', axis=0, tiled=True)  83.7 us
    all_gather x1, waiting for transfers between devices, per_device(): down_all = lax.all_gather(down_proj, 'fsdp', axis=2, tiled=True)  71.6 us
    all_gather x1, waiting for transfers between devices, per_device(): gate_all = lax.all_gather(gate_proj, 'fsdp', axis=1, tiled=True)  57.4 us
    all_gather x1, waiting for transfers between devices, per_device(): up_all = lax.all_gather(up_proj, 'fsdp', axis=1, tiled=True)  50.1 us
    dot_general x2, matrix products, per_device(): jnp.dot(act, down_all[e], preferred_element_type=jnp.float32)  47.9 us
    dot_general x2, matrix products, per_device(): gate = jnp.dot(tokens, gate_all[e], preferred_element_type=jnp.float32)  20.3 us
    all_to_all x1, blocking collectives, per_device(): lax.all_to_all(weights.reshape(weights.shape[0], lax.axis_size('ep'), loc...  11.8 us
  transfers between devices with their start and end apart: 5, of which 5 were waited for; matrix products, arithmetic and copies ran while one was open for 5% of the time, Pallas kernels for 0%

commit v1 on v0

--- a/solution.py
+++ b/solution.py
@@ -25,7 +25,14 @@
         tiled=True,
     ).reshape(tokens.shape[0], local_experts)
     total = 0.0
-    gate_all = lax.all_gather(gate_proj, "fsdp", axis=1, tiled=True)
+    size = lax.axis_size("fsdp")
+    right = [(i, (i + 1) % size) for i in range(size)]
+    parts = [gate_proj]
+    for far in range(1, size):
+        parts = [lax.ppermute(parts[0], "fsdp", right), *parts]
+    whole = jnp.concatenate(parts, axis=1)
+    offset = (lax.axis_index("fsdp") + 1) * parts[-1].shape[1]
+    gate_all = jnp.roll(whole, offset, axis=1)
     up_all = lax.all_gather(up_proj, "fsdp", axis=1, tiled=True)
     down_all = lax.all_gather(down_proj, "fsdp", axis=2, tiled=True)
     for e in range(local_experts):

time: 533 us -> 478 us (0.90)
  waiting for transfers between devices: 433 us -> 363 us
  local copies, waits for them, and re-layouts: 0.04 us -> 16.5 us
  blocking collectives: 11.8 us -> 0 us
  starting transfers between devices: 0.16 us -> 8.71 us
    ppermute x0 -> x3, waiting for transfers between devices: none -> 113 us  [per_device(): parts = [lax.ppermute(parts[0], 'fsdp', right), *parts]]
    all_gather x1, waiting for transfers between devices: 83.7 us -> 0.01 us  [per_device(): tokens = lax.all_gather(normed, 'ep', axis=0, tiled=True)]
    all_gather x1 -> x0, waiting for transfers between devices: 57.4 us -> none  [per_device(): gate_all = lax.all_gather(gate_proj, 'fsdp', axis=1, tiled=True)]
    all_gather x1, waiting for transfers between devices: 50.1 us -> 2.54 us  [per_device(): up_all = lax.all_gather(up_proj, 'fsdp', axis=1, tiled=True)]
    unnamed x8 -> x15, local copies, waits for them, and re-layouts: 0.01 us -> 14.6 us
    all_to_all x1 -> x0, blocking collectives: 11.8 us -> none  [per_device(): lax.all_to_all(weights.reshape(weights.shape[0], lax.axis_size('ep'), loc...]
    all_to_all x0 -> x1, waiting for transfers between devices: none -> 5.59 us  [per_device(): lax.all_to_all(weights.reshape(weights.shape[0], lax.axis_size('ep'), loc...]
  transfers between devices with their start and end apart: 5 -> 8, of which waited for: 5 -> 7; matrix products, arithmetic and copies ran while one was open for 5% -> 8% of each run, Pallas kernels for 0% -> 0%
where the time goes in v1:
time: 478 us
  waiting for transfers between devices  363 us (76%)
  matrix products  70 us (15%)
  local copies, waits for them, and re-layouts  16.5 us (3%)
  between operations  13.2 us (3%)
  starting transfers between devices  8.71 us (2%)
  other arithmetic  6.88 us (1%)
    reduce_scatter x1, waiting for transfers between devices, per_device(): combined = lax.psum_scatter(total, 'ep', scatter_dimension=0, tiled=True)  168 us
    ppermute x3, waiting for transfers between devices, per_device(): parts = [lax.ppermute(parts[0], 'fsdp', right), *parts]  113 us
    all_gather x1, waiting for transfers between devices, per_device(): down_all = lax.all_gather(down_proj, 'fsdp', axis=2, tiled=True)  71.8 us
    dot_general x2, matrix products, per_device(): jnp.dot(act, down_all[e], preferred_element_type=jnp.float32)  47.9 us
    dot_general x2, matrix products, per_device(): gate = jnp.dot(tokens, gate_all[e], preferred_element_type=jnp.float32)  22.1 us
    unnamed x15, local copies, waits for them, and re-layouts  14.6 us
  transfers between devices with their start and end apart: 8, of which 7 were waited for; matrix products, arithmetic and copies ran while one was open for 8% of the time, Pallas kernels for 0%

profile of v1, /device:TPU:0, one launch (start us, length us, event | category | flops | bytes accessed | tf_op | source)
XLA Modules:
  0.0 477.9 jit_solution(8513453567276228162)
XLA Ops:
  6.5 0.0 copy-start
  6.5 0.0 copy-start.1
  6.5 0.0 copy-start.2
  6.5 0.0 all-gather.4.cloned.1.call-start
  6.5 1.6 fusion.9
  8.2 2.5 fusion.11
  10.7 0.0 all-gather.4.cloned.1.call-update
  10.7 0.0 all-gather.6.cloned.1.call-start
  10.8 0.7 all-gather.6.cloned.1.call-update
  11.5 0.0 all-gather.8.cloned.1.call-start
  11.5 0.7 all-gather.8.cloned.1.call-update
  12.2 0.0 copy-done
  12.2 3.0 collective-permute-start
  15.2 35.3 %collective-permute-done = bf16[2,512,768]{2,1,0:T(8,128)(2,1)S(1)} collective-permute-done((bf16[2,512,768]{2,1,0:T(8,128)(2,1)S(1)}, bf16[2,512,768]{2,1,0:T(8,128)(2,1)S(1)}, u32[]{:S(2)}, u32[]{:S(2)}) %collective-permute-start) | collective-permute-done | bytes 1572896 | tf_op jit(solution)/shard_map/ppermute | solution.py:32
  50.6 0.8 collective-permute-start.1
  51.4 35.9 %collective-permute-done.1 = bf16[2,512,768]{2,1,0:T(8,128)(2,1)} collective-permute-done((bf16[2,512,768]{2,1,0:T(8,128)(2,1)S(1)}, bf16[2,512,768]{2,1,0:T(8,128)(2,1)}, u32[]{:S(2)}, u32[]{:S(2)}) %collective-permute-start.1) | collective-permute-done | bytes 1572896 | tf_op jit(solution)/shard_map/ppermute | solution.py:32
  87.2 0.0 collective-permute-start.2
  87.3 0.0 copy-done.1
  87.3 0.0 copy-done.2
  87.3 0.6 reshape.18
  87.9 4.8 %all-to-all-start = ((f32[256,8,2]{0,2,1:T(2,128)}), f32[256,8,2]{0,2,1:T(2,128)S(1)}, u32[]{:S(2)}, u32[]{:S(2)}) async-start(f32[256,8,2]{0,2,1:T(2,128)} %reshape.18), calls=%async_computation | async-start | bytes 32768 | tf_op jit(solution)/shard_map/all_to_all | solution.py:20
  92.7 0.0 reduce-scatter.2.cloned.1.call-start
  92.8 5.6 %all-to-all-done = f32[256,8,2]{0,2,1:T(2,128)S(1)} async-done(((f32[256,8,2]{0,2,1:T(2,128)}), f32[256,8,2]{0,2,1:T(2,128)S(1)}, u32[]{:S(2)}, u32[]{:S(2)}) %all-to-all-start) | async-done | bytes 16416 | tf_op jit(solution)/shard_map/all_to_all | solution.py:20
  98.4 41.8 %collective-permute-done.2 = bf16[2,512,768]{2,1,0:T(8,128)(2,1)} collective-permute-done((bf16[2,512,768]{2,1,0:T(8,128)(2,1)}, bf16[2,512,768]{2,1,0:T(8,128)(2,1)}, u32[]{:S(2)}, u32[]{:S(2)}) %collective-permute-start.2) | collective-permute-done | bytes 1572896 | tf_op jit(solution)/shard_map/ppermute | solution.py:32
  140.1 2.7 constant_dynamic-update-slice_fusion.7
  142.8 2.7 constant_dynamic-update-slice_fusion.6
  145.5 1.3 constant_dynamic-update-slice_fusion.5
  146.8 1.3 constant_dynamic-update-slice_fusion.4
  148.1 2.7 constant_dynamic-update-slice_fusion.3
  150.7 2.7 constant_dynamic-update-slice_fusion.2
  153.4 1.3 constant_dynamic-update-slice_fusion.1
  154.7 1.2 constant_dynamic-update-slice_fusion
  156.0 0.0 all-gather.4.cloned.1.call-done
  156.0 0.0 copy-start.3
  156.0 11.8 %fusion.5 = f32[2048,768]{1,0:T(8,128)} fusion(bf16[2048,2048]{1,0:T(8,128)(2,1)} %all-gather.4.cloned.1.call-done, bf16[2,4096,768]{2,1,0:T(8,128)(2,1)} %constant_dynamic-update-slice_fusion, s32[]{:T(128)S(6)} %add.44, s32[]{:T(128)S(6)} %select_n.18), kind=kOutput, calls=%fused_computation.9 | convolution fusion | flops 6442450944 | bytes 17825800 | tf_op jit(solution)/shard_map/dot_general | solution.py:39
  167.7 0.0 copy-done.3
  167.7 10.3 %fusion.6 = f32[2048,768]{1,0:T(8,128)} fusion(bf16[2048,2048]{1,0:T(8,128)(2,1)S(1)} %copy-done.3, bf16[2,4096,768]{2,1,0:T(8,128)(2,1)} %constant_dynamic-update-slice_fusion, s32[]{:T(128)S(6)} %select_n.18), kind=kOutput, calls=%fused_computation.13 | convolution fusion | flops 6442450944 | bytes 17825796 | tf_op jit(solution)/shard_map/dot_general | solution.py:39
  178.1 2.5 all-gather.6.cloned.1.call-done
  180.6 71.8 %all-gather.8.cloned.1.call-done = bf16[2,768,2048]{2,1,0:T(8,128)(2,1)} async-done(((bf16[2,768,512]{2,1,0:T(8,128)(2,1)}), bf16[2,768,2048]{2,1,0:T(8,128)(2,1)}) %all-gather.8.cloned.1.call-update) | async-done | bytes 6291472 | tf_op jit(solution)/shard_map/all_gather | solution.py:37
  252.4 22.2 %fusion = bf16[2048,2048]{1,0:T(8,128)(2,1)} fusion(f32[2048,768]{1,0:T(8,128)} %fusion.6, bf16[2048,2048]{1,0:T(8,128)(2,1)} %all-gather.4.cloned.1.call-done, bf16[2,768,2048]{2,1,0:T(8,128)(2,1)} %all-gather.8.cloned.1.call-done, bf16[2,2048,768]{2,1,0:T(8,128)(2,1)} %all-gather.6.cloned.1.call-done), kind=kOutput, calls=%fused_computation.3 | convolution fusion | flops 12894339072 | bytes 29360128 | tf_op jit(solution)/shard_map/dot_general | solution.py:42
  274.5 25.8 %multiply_add_fusion = f32[2048,2048]{1,0:T(8,128)} fusion(f32[2048]{0:T(1024)S(1)} %bitcast.35, f32[2048]{0:T(1024)S(1)} %bitcast.34, bf16[2048,2048]{1,0:T(8,128)(2,1)} %fusion, f32[2048,768]{1,0:T(8,128)} %fusion.5, bf16[2048,2048]{1,0:T(8,128)(2,1)} %all-gather.4.cloned.1.call-done, bf16[2,768,2048]{2,1,0:T(8,128)(2,1)} %all-gather.8.cloned.1.call-done, ...), kind=kOutput, calls=%fused_computation | convolution fusion | flops 12919504896 | bytes 46153728 | tf_op jit(solution)/shard_map/dot_general | solution.py:42
  300.3 0.0 reduce-scatter.2.cloned.1.call-update
  300.3 168.3 %reduce-scatter.2.cloned.1.call-done = f32[256,2048]{1,0:T(8,128)} async-done(((f32[2048,2048]{1,0:T(8,128)}), f32[256,2048]{1,0:T(8,128)}) %reduce-scatter.2.cloned.1.call-update) | async-done | bytes 2097168 | tf_op jit(solution)/shard_map/reduce_scatter | solution.py:44
  468.6 2.7 convert_element_type.35
  (3 shorter events, 0.0 us)
Async XLA Ops:
  6.5 5.7 %copy-start = (bf16[2,512,768]{2,1,0:T(8,128)(2,1)S(1)}, bf16[2,512,768]{2,1,0:T(8,128)(2,1)}, u32[]{:S(2)}) copy-start(bf16[2,512,768]{2,1,0:T(8,128)(2,1)} %param.11) | copy-start | bytes 4718596
  6.5 80.7 %copy-start.1 = (f32[256,8]{0,1:T(8,128)S(1)}, f32[256,8]{0,1:T(8,128)}, u32[]{:S(2)}) copy-start(f32[256,8]{0,1:T(8,128)} %param.10) | copy-start | bytes 24580
  6.5 80.7 %copy-start.2 = (s32[256,8]{0,1:T(8,128)S(1)}, s32[256,8]{0,1:T(8,128)}, u32[]{:S(2)}) copy-start(s32[256,8]{0,1:T(8,128)} %param.9) | copy-start | bytes 24580
  6.5 149.4 %all-gather.4.cloned.1.call-start = ((), (), s32[]{:S(2)}) async-start(), calls=%async_computation.2 | async-start | bytes 9437184 | tf_op jit(solution)/shard_map/all_gather | solution.py:19
  10.7 169.9 %all-gather.6.cloned.1.call-start = ((), (), s32[]{:S(2)}) async-start(), calls=%async_computation.3 | async-start | bytes 7864320 | tf_op jit(solution)/shard_map/all_gather | solution.py:36
  11.5 240.9 %all-gather.8.cloned.1.call-start = ((), (), s32[]{:S(2)}) async-start(), calls=%async_computation.4 | async-start | bytes 7864320 | tf_op jit(solution)/shard_map/all_gather | solution.py:37
  12.2 38.4 %collective-permute-start = (bf16[2,512,768]{2,1,0:T(8,128)(2,1)S(1)}, bf16[2,512,768]{2,1,0:T(8,128)(2,1)S(1)}, u32[]{:S(2)}, u32[]{:S(2)}) collective-permute-start(bf16[2,512,768]{2,1,0:T(8,128)(2,1)S(1)} %copy-done), channel_id=1, source_target_pairs={{0,8},{8,16},{16,24},{24,0},{1,9},{9,17},{17,25},{25,1},{2,10},{10... | collective-permute-start | bytes 4718600 | tf_op jit(solution)/shard_map/ppermute | solution.py:32
  50.6 36.7 %collective-permute-start.1 = (bf16[2,512,768]{2,1,0:T(8,128)(2,1)S(1)}, bf16[2,512,768]{2,1,0:T(8,128)(2,1)}, u32[]{:S(2)}, u32[]{:S(2)}) collective-permute-start(bf16[2,512,768]{2,1,0:T(8,128)(2,1)S(1)} %collective-permute-done), channel_id=1, source_target_pairs={{0,8},{8,16},{16,24},{24,0},{1,9},{9,17},{17,25},{25,1},{2,10},{10... | collective-permute-start | bytes 4718600 | tf_op jit(solution)/shard_map/ppermute | solution.py:32
  87.2 52.9 %collective-permute-start.2 = (bf16[2,512,768]{2,1,0:T(8,128)(2,1)}, bf16[2,512,768]{2,1,0:T(8,128)(2,1)}, u32[]{:S(2)}, u32[]{:S(2)}) collective-permute-start(bf16[2,512,768]{2,1,0:T(8,128)(2,1)} %collective-permute-done.1), channel_id=1, source_target_pairs={{0,8},{8,16},{16,24},{24,0},{1,9},{9,17},{17,25},{25,1},{2,10},{10... | collective-permute-start | bytes 4718600 | tf_op jit(solution)/shard_map/ppermute | solution.py:32
  87.9 10.4 %all-to-all-start = ((f32[256,8,2]{0,2,1:T(2,128)}), f32[256,8,2]{0,2,1:T(2,128)S(1)}, u32[]{:S(2)}, u32[]{:S(2)}) async-start(f32[256,8,2]{0,2,1:T(2,128)} %reshape.18), calls=%async_computation | async-start | bytes 32768 | tf_op jit(solution)/shard_map/all_to_all | solution.py:20
  92.7 375.9 %reduce-scatter.2.cloned.1.call-start = ((), (), s32[]{:S(2)}) async-start(), calls=%async_computation.5 | async-start | bytes 18874368 | tf_op jit(solution)/shard_map/reduce_scatter | solution.py:44
  156.0 11.8 %copy-start.3 = (bf16[2048,2048]{1,0:T(8,128)(2,1)S(1)}, bf16[2048,2048]{1,0:T(8,128)(2,1)}, u32[]{:S(2)}) copy-start(bf16[2048,2048]{1,0:T(8,128)(2,1)} %all-gather.4.cloned.1.call-done) | copy-start | bytes 25165828
Sparse Core Ops, SparseCore 0:
  10.8 84.7 all-gather.3
  97.5 83.1 all-gather.5
  182.5 69.8 all-gather.7
  300.4 168.1 reduce-scatter.1
